TPU v7x, 512 devices: a whole 4x8x8 slice. The times are simulated.
512 devices in a mesh: seq: 4 (over z_lo, core), exp: 32 (over x, y), ff: 4 (over z_hi).
Axes of the slice: x: 4, y: 8, z: 8 (z_hi: 4, z_lo: 2; z = z_hi * 2 + z_lo), core: 2. Of those that a mesh axis runs over, the one named last changes fastest.
Arguments:
- query_proj: bfloat16 [32, 512, 2560], P('exp', 'seq', 'ff'), may hold values from -85 to 85
- key_proj: bfloat16 [32, 512, 512], P('exp', 'seq', 'ff'), may hold values from -4.2 to 4.2
- value_proj: bfloat16 [32, 512, 512], P('exp', 'seq', 'ff'), may hold values from -6 to 6
- residual: bfloat16 [32, 512, 2560], P('exp', 'seq', 'ff'), may hold values from -60 to 60
- norm_gain: float32 [2560], P('ff'), may hold values from 0.5 to 2
- router_logit: float32 [32, 512], P('exp', 'seq'), may hold values from 1 to 6
- expert_ids: int32 [32, 512, 1], P('exp', 'seq'), may hold values from 0 to 31; in each aligned block of 128 rows (0 to 127, 128 to 255, ..., all dimensions but the last counted through in order) at most 6 rows name the same one
- gate_weight: bfloat16 [32, 2560, 4096], P('exp', None, ('seq', 'ff')), may hold values from -0.125 to 0.125
- up_weight: bfloat16 [32, 2560, 4096], P('exp', None, ('seq', 'ff')), may hold values from -0.125 to 0.125
- down_weight: bfloat16 [32, 4096, 2560], P('exp', ('seq', 'ff')), may hold values from -0.125 to 0.125
Outputs:
- layer_out: bfloat16 [32, 512, 2560], P('exp', 'seq', 'ff')
Inputs may be any that keep to these rules, and one draw needn't show every extreme that they name: `expert_ids`: within each aligned block of 128 positions of a span (the positions of one index of seq), no expert is named by more than 6 tokens, and in some blocks an expert is named by exactly 6.
All inputs are finite; a program needn't handle non-finite values.
Results may differ from a plain program's by a relative error of at most 0.015.
Values may be sent and summed in bfloat16 or wider, within the bound.
A program may use at most 64 MiB of HBM per device.

v0:
```python
import jax
import jax.numpy as jnp
from jax import lax
from jax.sharding import Mesh
from jax.sharding import PartitionSpec as P

HD = 128
HEADS = 20
KVH = 4
D = 2560
SEQ = ("seq_0", "seq_1")
SEQ_FF = ("seq_0", "seq_1", "ff")


floor_score = -1e30
norm_eps = 1e-05


def side_by_side(arrays, axis, dim, along):
    widths = [a.shape[along] for a in arrays]
    both = jnp.concatenate(arrays, axis=along)
    out = lax.all_gather(both, axis, axis=dim, tiled=True)
    return tuple(jnp.split(out, [sum(widths[:k]) for k in range(1, len(widths))], axis=along))


def sent_to_all(value, axis):
    copies = jnp.broadcast_to(value, (lax.axis_size(axis), *value.shape))
    return lax.all_to_all(copies, axis, split_axis=0, concat_axis=0, tiled=True)


def of_everyone(value, axis):
    everything = sent_to_all(value, axis)
    return jnp.sum(everything, axis=0)


def in_order(parts, dim):
    parts = jnp.moveaxis(parts, 0, dim)
    lengths = parts.shape
    return parts.reshape(*lengths[:dim], lengths[dim] * lengths[dim + 1], *lengths[dim + 2 :])


def gather_in_order(value, axes, sequence):
    parts = value
    for k in sequence:
        parts = lax.all_gather(parts, axes[k])
    done = sequence[::-1]
    back = [done.index(k) for k in range(len(axes))]
    parts = parts.transpose(*back, *range(len(axes), parts.ndim))
    return parts.reshape(-1, *value.shape)


def whole_of(value, axes, sequence, dim):
    return in_order(gather_in_order(value, axes, sequence), dim)


def fold_block(carry, queries, first, keys_in, values_in):
    running_max, running_sum, accumulated = carry
    kv_local = queries.shape[1]
    key_rows = keys_in.reshape(keys_in.shape[0], kv_local, HD)
    value_rows = values_in.reshape(values_in.shape[0], kv_local, HD)
    scores = jnp.einsum(
        "qagd,kad->agqk", queries, key_rows, preferred_element_type=jnp.float32
    ) * HD ** (-0.5)
    query_pos = first + lax.iota(jnp.int32, queries.shape[0])
    key_pos = lax.iota(jnp.int32, keys_in.shape[0])
    allowed = (key_pos[None, :] <= query_pos[:, None]) & (key_pos[None, :] >= 0)
    masked = jnp.where(allowed, scores, floor_score)
    new_max = jnp.maximum(running_max, jnp.max(masked, axis=-1))
    weights = jnp.where(allowed, jnp.exp(masked - new_max[..., None]), 0.0)
    running_sum = jnp.sum(weights, axis=-1)
    accumulated = jnp.einsum(
        "agqk,kad->agqd",
        weights.astype(jnp.bfloat16),
        value_rows,
        preferred_element_type=jnp.float32,
    )
    return (new_max, running_sum, accumulated)


def body(
    query_proj,
    key_proj,
    value_proj,
    residual,
    norm_gain,
    router_logit,
    expert_ids,
    gate_weight,
    up_weight,
    down_weight,
):
    shard_len = query_proj.shape[1]
    kv_local = key_proj.shape[2] // HD
    group = HEADS // KVH
    queries = query_proj[0].reshape(shard_len, kv_local, group, HD)
    first = lax.axis_index(SEQ) * shard_len
    initial = (
        jnp.full((kv_local, group, shard_len), floor_score, jnp.float32),
        jnp.zeros((kv_local, group, shard_len), jnp.float32),
        jnp.zeros((kv_local, group, shard_len, HD), jnp.float32),
    )
    piece = side_by_side((key_proj[0], value_proj[0]), SEQ, 0, 1)
    carry = fold_block(initial, queries, first, piece[0], piece[1])
    attention = carry[2] / carry[1][..., None]
    attention = attention.transpose(2, 0, 1, 3).reshape(shard_len, kv_local * group * HD)
    stream = (residual[0].astype(jnp.float32) + attention).astype(jnp.bfloat16)
    stream_f = stream.astype(jnp.float32)
    squares = of_everyone(jnp.sum(stream_f * stream_f, axis=1), "ff")
    inverse = lax.rsqrt(squares / D + norm_eps)
    routed_in = (
        stream_f * inverse[:, None] * norm_gain[None, :] * jax.nn.sigmoid(router_logit[0])[:, None]
    )
    routed_in = routed_in.astype(jnp.bfloat16)
    expert_count = lax.axis_size("exp")
    seq_count = lax.axis_size(SEQ)
    ff_count = lax.axis_size("ff")
    capacity = max(2, 3 * shard_len // (2 * expert_count))
    route = expert_ids[0, :, 0]
    onehot = (route[:, None] == lax.iota(jnp.int32, expert_count)[None, :]).astype(jnp.bfloat16)
    row_iota = lax.iota(jnp.int32, shard_len)
    below = (row_iota[:, None] > row_iota[None, :]).astype(jnp.bfloat16)
    earlier = jnp.dot(below, onehot, preferred_element_type=jnp.float32)
    slot = jnp.sum(earlier * onehot.astype(jnp.float32), axis=1).astype(jnp.int32)
    target = route * capacity + slot
    selector = (target[:, None] == lax.iota(jnp.int32, expert_count * capacity)[None, :]).astype(
        jnp.bfloat16
    )
    outgoing = jnp.einsum(
        "tr,tc->rc", selector, routed_in, preferred_element_type=jnp.float32
    ).astype(jnp.bfloat16)
    quarter = D // ff_count
    width_here = gate_weight.shape[2]
    gate_parts = gate_weight[0].reshape(ff_count, quarter, width_here)
    up_parts = up_weight[0].reshape(ff_count, quarter, width_here)
    incoming = lax.all_to_all(outgoing, "exp", split_axis=0, concat_axis=0, tiled=True)
    everyone = whole_of(incoming, SEQ_FF, (2, 0, 1), 0)
    blocks = everyone.reshape(seq_count, ff_count, -1, quarter)
    gate = jnp.einsum("sfjc,fck->sjk", blocks, gate_parts, preferred_element_type=jnp.float32)
    upward = jnp.einsum("sfjc,fck->sjk", blocks, up_parts, preferred_element_type=jnp.float32)
    activated = (jax.nn.silu(gate) * upward).astype(jnp.bfloat16)
    down_parts = down_weight[0].reshape(width_here, ff_count, quarter)
    term = jnp.einsum("sjk,kfc->sfjc", activated, down_parts, preferred_element_type=jnp.float32)
    summed = lax.psum_scatter(
        term.reshape(-1, quarter).astype(jnp.bfloat16), SEQ_FF, scatter_dimension=0, tiled=True
    )
    returned = lax.all_to_all(summed, "exp", split_axis=0, concat_axis=0, tiled=True)
    combined = jnp.dot(selector, returned, preferred_element_type=jnp.float32)
    return (stream_f + combined).astype(jnp.bfloat16)[None]


def solution(mesh):
    torus = Mesh(
        mesh.devices.reshape(2, 2, mesh.shape["exp"], mesh.shape["ff"]),
        ("seq_0", "seq_1", "exp", "ff"),
    )
    placed = (
        P("exp", SEQ, "ff"),
        P("exp", SEQ, "ff"),
        P("exp", SEQ, "ff"),
        P("exp", SEQ, "ff"),
        P("ff"),
        P("exp", SEQ),
        P("exp", SEQ, None),
        P("exp", None, SEQ_FF),
        P("exp", None, SEQ_FF),
        P("exp", SEQ_FF, None),
    )
    return jax.shard_map(
        body, mesh=torus, in_specs=placed, out_specs=P("exp", SEQ, "ff"), check_vma=False
    )
```

profile of v0, /device:TPU:6, one launch (start us, length us, event | category | flops | bytes accessed | tf_op | source)
XLA Modules:
  0.0 283.1 jit_solution(5798929004068213681)
XLA Ops:
  6.5 0.0 copy-start
  6.5 0.1 iota_compare_fusion
  6.6 1.2 copy.41
  7.8 0.8 pad_maximum_fusion
  8.6 6.6 %all_gather.21 = bf16[512,256]{1,0:T(8,128)(2,1)S(1)} all-gather(bf16[128,256]{1,0:T(8,128)(2,1)S(1)} %pad_maximum_fusion), channel_id=1, replica_groups=mesh['seq_0'=2,'seq_1'=2,'exp'=32,'ff'=4] {'seq_0','seq_1'}, dimensions={0}, use_global_device_ids=true | all-gather | bytes 327680 | tf_op jit(solution)/shard_map/all_gather | solution.py:22
  15.2 1.0 copy.46
  16.2 0.3 fusion.39
  16.6 0.2 fusion.10
  16.8 0.0 copy-start.7
  16.8 0.0 copy-start.8
  16.9 0.0 copy-start.2
  16.9 0.0 copy-start.5
  16.9 0.4 multiply_reduce_fusion
  17.3 0.6 broadcast_in_dim.38
  17.9 9.5 %all-to-all-start = ((f32[4,1,128]{2,1,0:T(1,128)}), f32[4,1,128]{2,1,0:T(1,128)S(1)}, u32[]{:S(2)}, u32[]{:S(2)}) async-start(f32[4,1,128]{2,1,0:T(1,128)} %broadcast_in_dim.38), calls=%async_computation | async-start | bytes 4096 | tf_op jit(solution)/shard_map/all_to_all | solution.py:28
  27.4 0.0 all-gather.5.cloned.1.call-start
  27.4 0.0 copy-done.7
  27.4 0.2 fusion.9
  27.5 0.0 copy-done.8
  27.6 0.2 copy.45
  27.7 7.2 %all-to-all-done = f32[4,1,128]{2,1,0:T(1,128)S(1)} async-done(((f32[4,1,128]{2,1,0:T(1,128)}), f32[4,1,128]{2,1,0:T(1,128)S(1)}, u32[]{:S(2)}, u32[]{:S(2)}) %all-to-all-start) | async-done | bytes 2080 | tf_op jit(solution)/shard_map/all_to_all | solution.py:28
  35.0 0.0 copy-done.2
  35.0 0.0 copy-done.5
  35.0 0.3 convolution_convert_fusion.1
  35.4 0.1 all_to_all.19
  35.5 20.7 %all_to_all.27 = bf16[32,6,640]{2,1,0:T(8,128)(2,1)S(1)} all-to-all(bf16[32,6,640]{2,1,0:T(8,128)(2,1)S(1)} %all_to_all.19), channel_id=1, replica_groups=mesh['seq_0'=2,'seq_1'=2,'exp'=32,'ff'=4] {'exp'}, dimensions={0} | all-to-all | bytes 491520 | tf_op jit(solution)/shard_map/all_to_all | solution.py:135
  56.1 0.1 all_gather.22
  56.2 19.0 %all_gather.23 = bf16[4,192,640]{2,1,0:T(8,128)(2,1)} all-gather(bf16[1,192,640]{2,1,0:T(8,128)(2,1)S(1)} %all_gather.22), channel_id=1, replica_groups=mesh['seq_0'=2,'seq_1'=2,'exp'=32,'ff'=4] {'ff'}, dimensions={0}, use_global_device_ids=true | all-gather | bytes 1228800 | tf_op jit(solution)/shard_map/all_gather | solution.py:45
  75.2 0.0 copy-start.3
  75.2 0.0 all-gather.5.cloned.1.call-update
  75.2 0.0 all-gather.7.cloned.1.call-start
  75.3 37.7 %all-gather.5.cloned.1.call-done = bf16[8,192,640]{2,1,0:T(8,128)(2,1)} async-done(((bf16[4,192,640]{2,1,0:T(8,128)(2,1)}), bf16[8,192,640]{2,1,0:T(8,128)(2,1)}) %all-gather.5.cloned.1.call-update) | async-done | bytes 1966096 | tf_op jit(solution)/shard_map/all_gather | solution.py:45
  113.0 0.0 all-gather.7.cloned.1.call-update
  113.0 0.0 reduce-scatter.2.cloned.1.call-start
  113.0 0.0 copy-done.3
  113.1 1.3 reshape_squeeze.12
  114.3 22.6 %all-gather.7.cloned.1.call-done = bf16[4,4,192,640]{3,2,1,0:T(8,128)(2,1)} async-done(((bf16[2,4,192,640]{3,2,1,0:T(8,128)(2,1)}), bf16[4,4,192,640]{3,2,1,0:T(8,128)(2,1)}) %all-gather.7.cloned.1.call-update) | async-done | bytes 3932176 | tf_op jit(solution)/shard_map/all_gather | solution.py:45
  136.9 0.0 copy-start.6
  136.9 2.6 copy.48
  139.5 0.0 copy-start.1
  139.5 0.0 copy-done.6
  139.5 0.0 copy-start.4
  139.5 2.1 convolution_bitcast_fusion.1
  141.7 0.0 copy-done.1
  141.7 0.0 copy-done
  141.7 0.2 copy-done.4
  141.8 8.3 %convolution_convert_fusion = bf16[4,192,4,640]{3,1,2,0:T(8,128)(2,1)} fusion(bf16[256,4,640]{2,1,0:T(4,128)(2,1)S(1)} %copy-done.4, bf16[4,4,192,640]{3,2,1,0:T(8,128)(2,1)} %bitcast.98, bf16[4,640,256,1]{2,1,0,3:T(8,128)(2,1)S(1)} %bitcast.94, f32[4,192,256]{2,1,0:T(8,128)} %convolution_bitcast_fusion.1), kind=kOutput, calls=%fused_computation | convolution fusion | flops 2016411648 | bytes 11272192 | tf_op jit(solution)/shard_map/sjk,kfc->sfjc/dot_general | solution.py:142
  150.2 0.0 reduce-scatter.2.cloned.1.call-update
  150.2 101.9 %reduce-scatter.2.cloned.1.call-done = bf16[192,640]{1,0:T(8,128)(2,1)} async-done(((bf16[3072,640]{1,0:T(8,128)(2,1)}), bf16[192,640]{1,0:T(8,128)(2,1)}) %reduce-scatter.2.cloned.1.call-update) | async-done | bytes 245776 | tf_op jit(solution)/shard_map/reduce_scatter | solution.py:143
  252.1 1.0 all_to_all.21
  253.1 22.5 %all_to_all.28 = bf16[32,6,640]{2,1,0:T(8,128)(2,1)S(1)} all-to-all(bf16[32,6,640]{2,1,0:T(8,128)(2,1)S(1)} %all_to_all.21), channel_id=1, replica_groups=mesh['seq_0'=2,'seq_1'=2,'exp'=32,'ff'=4] {'exp'}, dimensions={0} | all-to-all | bytes 491520 | tf_op jit(solution)/shard_map/all_to_all | solution.py:146
  275.5 0.1 all_to_all.23
  275.6 0.9 fusion.8
  (6 shorter events, 0.1 us)
Async XLA Ops:
  6.5 135.1 %copy-start = (bf16[1,2560,256]{2,1,0:T(8,128)(2,1)S(1)}, bf16[1,2560,256]{2,1,0:T(8,128)(2,1)}, u32[]{:S(2)}) copy-start(bf16[1,2560,256]{2,1,0:T(8,128)(2,1)} %param.18) | copy-start | bytes 3932164
  16.8 10.5 %copy-start.7 = (s32[1,128,1]{1,2,0:T(1,128)S(1)}, s32[1,128,1]{1,2,0:T(1,128)}, u32[]{:S(2)}) copy-start(s32[1,128,1]{1,2,0:T(1,128)} %param.16) | copy-start | bytes 1540
  16.8 10.7 %copy-start.8 = (f32[1,128]{1,0:T(1,128)S(1)}, f32[1,128]{1,0:T(1,128)}, u32[]{:S(2)}) copy-start(f32[1,128]{1,0:T(1,128)} %param.15) | copy-start | bytes 1540
  16.9 18.2 %copy-start.2 = (bf16[1,128,640]{2,1,0:T(8,128)(2,1)S(1)}, bf16[1,128,640]{2,1,0:T(8,128)(2,1)}, u32[]{:S(2)}) copy-start(bf16[1,128,640]{2,1,0:T(8,128)(2,1)} %param.13) | copy-start | bytes 491524
  16.9 18.1 %copy-start.5 = (f32[640]{0:T(1024)S(1)}, f32[640]{0:T(1024)}, u32[]{:S(2)}) copy-start(f32[640]{0:T(1024)} %param.14) | copy-start | bytes 7684
  17.9 17.1 %all-to-all-start = ((f32[4,1,128]{2,1,0:T(1,128)}), f32[4,1,128]{2,1,0:T(1,128)S(1)}, u32[]{:S(2)}, u32[]{:S(2)}) async-start(f32[4,1,128]{2,1,0:T(1,128)} %broadcast_in_dim.38), calls=%async_computation | async-start | bytes 4096 | tf_op jit(solution)/shard_map/all_to_all | solution.py:28
  27.4 85.6 %all-gather.5.cloned.1.call-start = ((), (), s32[]{:S(2)}) async-start(), calls=%async_computation.5 | async-start | bytes 2949120 | tf_op jit(solution)/shard_map/all_gather | solution.py:45
  75.2 37.8 %copy-start.3 = (bf16[1,256,2560]{2,1,0:T(8,128)(2,1)S(1)}, bf16[1,256,2560]{2,1,0:T(8,128)(2,1)}, u32[]{:S(2)}) copy-start(bf16[1,256,2560]{2,1,0:T(8,128)(2,1)} %param.19) | copy-start | bytes 3932164
  75.2 61.7 %all-gather.7.cloned.1.call-start = ((), (), s32[]{:S(2)}) async-start(), calls=%async_computation.6 | async-start | bytes 5898240 | tf_op jit(solution)/shard_map/all_gather | solution.py:45
  113.0 139.1 %reduce-scatter.2.cloned.1.call-start = ((), (), s32[]{:S(2)}) async-start(), calls=%async_computation.4 | async-start | bytes 4177920 | tf_op jit(solution)/shard_map/reduce_scatter | solution.py:143
  136.9 2.6 copy-start.6
  139.5 2.2 copy-start.1
  139.5 2.3 copy-start.4
Sparse Core Ops, SparseCore 0:
  75.4 37.5 all-gather.4
  115.1 21.8 all-gather.6
  150.3 101.6 reduce-scatter.1
where the time goes:
time: 285 us; the launch traced here: 283 us
  waiting for transfers between devices  169 us (59%)
  blocking collectives  68.7 us (24%)
  between operations  13.3 us (5%)
  matrix products  12.7 us (4%)
  starting transfers between devices  9.53 us (3%)
  local copies, waits for them, and re-layouts  8.29 us (3%)
    reduce_scatter x1, waiting for transfers between devices, body(): lax.psum_scatter(term.reshape(-1, quarter).astype(jnp.bfloat16), SEQ_FF,...  102 us
    all_gather x2, waiting for transfers between devices, gather_in_order(): parts = lax.all_gather(parts, axes[k])  60.3 us
    all_to_all x1, blocking collectives, body(): lax.all_to_all(summed, 'exp', split_axis=0, concat_axis=0, tiled=True)  22.5 us
    all_to_all x1, blocking collectives, body(): lax.all_to_all(outgoing, 'exp', split_axis=0, concat_axis=0, tiled=True)  20.7 us
    all_gather x1, blocking collectives, gather_in_order(): parts = lax.all_gather(parts, axes[k])  19 us
    all_to_all x1, starting transfers between devices, sent_to_all(): return lax.all_to_all(copies, axis, split_axis=0, concat_axis=0, tiled=True)  9.45 us
    dot_general x1, matrix products, body(): jnp.einsum('sjk,kfc->sfjc', activated, down_parts, preferred_element_type...  8.35 us
    all_to_all x1, waiting for transfers between devices, sent_to_all(): return lax.all_to_all(copies, axis, split_axis=0, concat_axis=0, tiled=True)  7.25 us
  transfers between devices with their start and end apart: 4, of which 4 were waited for; matrix products, arithmetic and copies ran while one was open for 1% of the time, Pallas kernels for 0%

commit v1 on v0

v1 whole, which is shorter than its diff:
```python
import jax
import jax.numpy as jnp
from jax import lax
from jax.experimental import pallas as pl
from jax.experimental.pallas import tpu as pltpu
from jax.sharding import Mesh
from jax.sharding import PartitionSpec as P

HD = 128
HEADS = 20
KVH = 4
D = 2560
CAP = 6
PAD = 8
SEQ = ("zl", "core")
SEQ_FF = ("zl", "core", "ff")
NORM_EPS = 1e-05
FLOOR = -1e30
BF16 = jnp.bfloat16
F32 = jnp.float32
MESH = pl.DeviceIdType.MESH


def remote(src, dst, send, recv, where):
    return pltpu.make_async_remote_copy(
        src_ref=src, dst_ref=dst, send_sem=send, recv_sem=recv, device_id=where, device_id_type=MESH
    )


def dot(a, b):
    return jnp.dot(a, b, preferred_element_type=F32)


def dot_rows(a, b):
    return lax.dot_general(a, b, (((0,), (0,)), ((), ())), preferred_element_type=F32)


def dot_cols(a, b):
    return lax.dot_general(a, b, (((1,), (1,)), ((), ())), preferred_element_type=F32)


def iota(shape, dim):
    return lax.broadcasted_iota(jnp.int32, shape, dim)


def as_column(row):
    n = row.shape[-1]
    eye = iota((n, n), 0) == iota((n, n), 1)
    return jnp.sum(jnp.where(eye, jnp.broadcast_to(row, (n, n)), 0.0), axis=1, keepdims=True)


def kv_kernel(k_ref, v_ref, k_out, v_out, send_sem, recv_sem):
    zl, core = lax.axis_index("zl"), lax.axis_index("core")
    me = zl * 2 + core
    peers = (
        {"zl": 1 - zl, "core": core},
        {"zl": 1 - zl, "core": 1 - core},
        {"core": 1 - core},
    )
    barrier = pltpu.get_barrier_semaphore()
    for where in peers:
        pl.semaphore_signal(barrier, inc=1, device_id=where, device_id_type=MESH)
    k_out[me] = k_ref[...]
    v_out[me] = v_ref[...]
    pl.semaphore_wait(barrier, 3)
    copies = []
    for n, (src, dst) in enumerate(((k_ref, k_out), (v_ref, v_out))):
        for p, where in enumerate(peers):
            copies.append(remote(src, dst.at[me], send_sem.at[n, p], recv_sem.at[n, p], where))
            copies[-1].start()
    for copy in copies:
        copy.wait()


def gather_kv(key, value):
    rows, width = key.shape
    vmem = pl.BlockSpec(memory_space=pltpu.VMEM)
    shape = jax.ShapeDtypeStruct((4, rows, width), key.dtype)
    return pl.pallas_call(
        kv_kernel,
        out_shape=(shape, shape),
        in_specs=[vmem] * 2,
        out_specs=(vmem, vmem),
        scratch_shapes=[pltpu.SemaphoreType.DMA((2, 3)), pltpu.SemaphoreType.DMA((2, 3))],
        compiler_params=pltpu.CompilerParams(collective_id=0, has_side_effects=True),
        name="gather_kv",
    )(key, value)


def layer_kernel(
    n_exp,
    n_ff,
    q_ref,
    k_ref,
    v_ref,
    res_ref,
    gain_ref,
    logit_ref,
    ids_ref,
    wg_hbm,
    wu_hbm,
    wd_hbm,
    out_ref,
    wg_raw,
    wu_raw,
    wd,
    wgu,
    stream,
    sel,
    packed,
    landed,
    gains,
    sigs,
    xbuf,
    acc,
    sq,
    act,
    sib_out,
    sib_in,
    rs_out,
    rs_in,
    back_out,
    back_in,
    w_sem,
    gain_send,
    gain_recv,
    a2a_send,
    a2a_recv,
    sig_send,
    sig_recv,
    ag_send,
    ag_recv,
    own_send,
    own_recv,
    fwd_send,
    fwd_recv,
    sp_send,
    sp_recv,
    rs_send,
    rs_recv,
    bk_send,
    bk_recv,
):
    n_ring = 2 * n_ff
    items = n_ring - 1
    zl, core = lax.axis_index("zl"), lax.axis_index("core")
    exp, ff = lax.axis_index("exp"), lax.axis_index("ff")
    shard = zl * 2 + core
    zeta = ff * 2 + zl
    tokens, width = q_ref.shape
    slots = n_exp * PAD
    rows = n_exp * CAP
    half = rows // 2
    hidden = wg_raw.shape[1]

    def at_ring(step):
        z = lax.rem(zeta + step + n_ring, n_ring)
        return {"zl": lax.rem(z, 2), "ff": z // 2}

    sibling = {"core": 1 - core}
    seq_peers = (sibling, {"zl": 1 - zl}, {"zl": 1 - zl, "core": 1 - core})
    nxt = (at_ring(1), at_ring(-1))

    barrier = pltpu.get_barrier_semaphore()

    def greet(k, carry):
        pl.semaphore_signal(
            barrier, inc=1, device_id={"exp": lax.rem(exp + k, n_exp)}, device_id_type=MESH
        )
        return carry

    lax.fori_loop(1, n_exp, greet, 0)
    greeted = [sibling, {"zl": 1 - zl, "core": 1 - core}, *nxt]
    ff_peers = [{"ff": lax.rem(ff + k, n_ff)} for k in range(1, n_ff)]
    for where in greeted + ff_peers:
        pl.semaphore_signal(barrier, inc=1, device_id=where, device_id_type=MESH)

    loads = [
        pltpu.make_async_copy(src, dst, w_sem.at[n])
        for n, (src, dst) in enumerate(((wg_hbm, wg_raw), (wu_hbm, wu_raw), (wd_hbm, wd)))
    ]
    for load in loads:
        load.start()

    kv_local = k_ref.shape[2] // HD
    group = HEADS // KVH
    span = 4 * tokens
    for a in range(kv_local):
        keys = k_ref[:, :, a * HD : (a + 1) * HD].reshape(span, HD)
        values = v_ref[:, :, a * HD : (a + 1) * HD].reshape(span, HD)
        allowed = iota((tokens, span), 1) <= iota((tokens, span), 0) + shard * tokens
        for g in range(group):
            h = (a * group + g) * HD
            scores = dot_cols(q_ref[:, h : h + HD], keys) * HD ** (-0.5)
            scores = jnp.where(allowed, scores, FLOOR)
            peak = jnp.max(scores, axis=-1, keepdims=True)
            weights = jnp.where(allowed, jnp.exp(scores - peak), 0.0)
            total = jnp.sum(weights, axis=-1, keepdims=True)
            mixed = dot(weights.astype(BF16), values) / total
            stream[:, h : h + HD] = (res_ref[:, h : h + HD].astype(F32) + mixed).astype(BF16)

    route = as_column(ids_ref[...].astype(F32))
    onehot = (route == iota((tokens, HD), 1).astype(F32)).astype(F32)
    below = (iota((tokens, tokens), 0) > iota((tokens, tokens), 1)).astype(BF16)
    earlier = dot(below, onehot.astype(BF16))
    slot = jnp.sum(earlier * onehot, axis=1, keepdims=True)
    lane = iota((tokens, slots), 1).astype(F32)
    pick = (lane == route * PAD + slot).astype(BF16)
    sel[...] = pick
    gate_in = as_column(jax.nn.sigmoid(logit_ref[...]))
    gate_hi = gate_in.astype(BF16)
    gate_lo = (gate_in - gate_hi.astype(F32)).astype(BF16)
    at_slot = slot == iota((tokens, HD), 1).astype(F32)
    meta = dot_rows(
        (lane == route * PAD + CAP).astype(BF16), jnp.where(at_slot, gate_hi.astype(F32), 0.0).astype(BF16)
    ) + dot_rows(
        (lane == route * PAD + (CAP + 1)).astype(BF16),
        jnp.where(at_slot, gate_lo.astype(F32), 0.0).astype(BF16),
    )
    for c in range(0, width, HD):
        block = dot_rows(pick, stream[:, c : c + HD])
        if c == 0:
            block = block + meta
        packed[:, :, c : c + HD] = block.astype(BF16).reshape(n_exp, PAD, HD)
    landed[exp] = packed[exp]
    gains[ff] = gain_ref[...]
    acc[...] = jnp.zeros_like(acc)
    sq[...] = jnp.zeros_like(sq)

    pl.semaphore_wait(barrier, n_exp - 1 + len(greeted) + len(ff_peers))

    def gain_copy(k):
        return remote(
            gains.at[ff], gains.at[ff], gain_send.at[k], gain_recv.at[k], ff_peers[k]
        )

    for k in range(n_ff - 1):
        gain_copy(k).start()

    def a2a_copy(k):
        to = lax.rem(exp + k, n_exp)
        return remote(
            packed.at[to], landed.at[exp], a2a_send.at[k - 1], a2a_recv.at[k - 1], {"exp": to}
        )

    def a2a_start(k, carry):
        a2a_copy(k).start()
        return carry

    lax.fori_loop(1, n_exp, a2a_start, 0)

    for load in loads:
        load.wait()
    for k in range(n_ff - 1):
        gain_copy(k).wait_recv()

    cols = width // HD

    def fold(b, carry):
        f = b // cols
        r = b - f * cols
        column = as_column(gains[f, pl.ds(r, 1), :])
        src = pl.ds(pl.multiple_of(b * HD, HD), HD)
        dst = pl.ds(pl.multiple_of(r * HD, HD), HD)
        wgu[f, dst, 0:hidden] = (wg_raw[src, :].astype(F32) * column).astype(BF16)
        wgu[f, dst, hidden : 2 * hidden] = (wu_raw[src, :].astype(F32) * column).astype(BF16)
        return carry

    lax.fori_loop(0, n_ff * cols, fold, 0)

    def a2a_wait(k, carry):
        a2a_copy(k).wait_recv()
        return carry

    lax.fori_loop(1, n_exp, a2a_wait, 0)

    q_col = iota((rows, slots), 1)
    keep = (iota((rows, slots), 0) == q_col - 2 * (q_col >> 3)) & ((q_col & 7) < CAP)
    keep = keep.astype(BF16)
    for c in range(0, width, HD):
        whole = landed[:, :, c : c + HD].reshape(slots, HD)
        dense = dot(keep, whole).astype(BF16)
        xbuf[zeta, core, 0, :, c : c + HD] = dense[:half]
        xbuf[zeta, core, 1, :, c : c + HD] = dense[half:]
        if c == 0:
            q_m = iota((2 * n_exp, slots), 1)
            pick_m = (iota((2 * n_exp, slots), 0) == (q_m >> 3) * 2 + (q_m & 7) - CAP) & ((q_m & 7) >= CAP)
            sigs[shard] = dot(pick_m.astype(BF16), whole).astype(BF16)

    def ring_item(d, j):
        z = zeta - (j // 2 + 1) if d == 0 else zeta + (j // 2 + 1)
        z = lax.rem(z + n_ring, n_ring)
        h = lax.rem(j, 2) if d == 0 else 1 - lax.rem(j, 2)
        return z, h

    def ag_copy(d, j, z, h):
        return remote(
            xbuf.at[z, core, h], xbuf.at[z, core, h], ag_send.at[d, j], ag_recv.at[d, j], nxt[d]
        )

    def own_copy(h):
        return remote(
            xbuf.at[zeta, core, h], xbuf.at[zeta, core, h], own_send.at[h], own_recv.at[h], sibling
        )

    def fwd_copy(d, j, z, h):
        return remote(
            xbuf.at[z, core, h], xbuf.at[z, core, h], fwd_send.at[d, j], fwd_recv.at[d, j], sibling
        )

    def sib_fwd(d, j, z, h):
        return remote(
            xbuf.at[z, 1 - core, h], xbuf.at[z, 1 - core, h], fwd_send.at[d, j], fwd_recv.at[d, j], sibling
        )

    for n in range(2):
        for d in range(2):
            ag_copy(d, n, zeta, n if d == 0 else 1 - n).start()
    for h in range(2):
        own_copy(h).start()
    sig_copies = [
        remote(sigs.at[shard], sigs.at[shard], sig_send.at[p], sig_recv.at[p], where)
        for p, where in enumerate(seq_peers)
    ]
    for copy in sig_copies:
        copy.start()

    def multiply(z, c, h):
        x = xbuf[z, c, h]
        s = lax.rem(z, 2) * 2 + c
        acc[s, h] += dot(x, wgu[z // 2])
        squares = None
        for b in range(cols):
            xf = x[:, b * HD : (b + 1) * HD].astype(F32)
            squares = xf * xf if squares is None else squares + xf * xf
        sq[s, h] += squares

    for h in range(2):
        multiply(zeta, core, h)
    for h in range(2):
        remote(
            xbuf.at[zeta, 1 - core, h], xbuf.at[zeta, 1 - core, h], own_send.at[h], own_recv.at[h], sibling
        ).wait_recv()
    for h in range(2):
        multiply(zeta, 1 - core, h)

    def gather_step(j, carry):
        for d in range(2):
            z, h = ring_item(d, j)
            ag_copy(d, j, z, h).wait_recv()

            @pl.when(j < items - 2)
            def _():
                ag_copy(d, j + 2, z, h).start()

            fwd_copy(d, j, z, h).start()
        for d in range(2):
            z, h = ring_item(d, j)
            multiply(z, core, h)
        for d in range(2):
            z, h = ring_item(d, j)
            sib_fwd(d, j, z, h).wait_recv()
            multiply(z, 1 - core, h)
        return carry

    lax.fori_loop(0, items, gather_step, 0)

    for copy in sig_copies:
        copy.wait_recv()

    for h in range(2):
        r_row = iota((half, 2 * n_exp), 0) + h * half
        first = 6 * (iota((half, 2 * n_exp), 1) >> 1)
        spread = ((r_row >= first) & (r_row < first + CAP)).astype(BF16)
        r_lane = iota((half, HD), 0) + h * half
        r_slot = r_lane - CAP * ((r_lane * 683) >> 12)
        here = r_slot == iota((half, HD), 1)
        for s in range(4):
            sig = jnp.sum(jnp.where(here, dot(spread, sigs[s]), 0.0), axis=1, keepdims=True)
            meansq = jnp.sum(sq[s, h], axis=1, keepdims=True) / D
            factor = lax.rsqrt(meansq + NORM_EPS) * sig
            gate = acc[s, h, :, 0:hidden] * factor
            up = acc[s, h, :, hidden : 2 * hidden] * factor
            act[s, h] = (gate / (1.0 + jnp.exp(-gate)) * up).astype(BF16)

    def partial(z, c, h):
        s = lax.rem(z, 2) * 2 + c
        return dot(act[s, h], wd[:, pl.ds(pl.multiple_of((z // 2) * width, HD), width)])

    def rs_target(d, j):
        k = n_ff - (j + 1) // 2
        z = lax.rem((zeta + k if d == 0 else zeta - k) + n_ring, n_ring)
        h = lax.rem(j, 2) if d == 0 else 1 - lax.rem(j, 2)
        return z, h

    def sp_copy(d, j):
        return remote(
            sib_out.at[d, j], sib_in.at[d, j], sp_send.at[d, j], sp_recv.at[d, j], sibling
        )

    def for_sibling(j):
        for d in range(2):
            z, h = rs_target(d, j)
            sib_out[d, j] = partial(z, 1 - core, h).astype(BF16)
        for d in range(2):
            sp_copy(d, j).start()

    def rs_copy(d, j):
        return remote(rs_out.at[d, j], rs_in.at[d, j], rs_send.at[d, j], rs_recv.at[d, j], nxt[d])

    def scatter_step(j, carry):
        @pl.when(j < items - 1)
        def _():
            for_sibling(j + 1)

        for d in range(2):
            z, h = rs_target(d, j)
            mine = partial(z, core, h)
            sp_copy(d, j).wait_recv()
            rs_out[d, j] = (mine + sib_in[d, j].astype(F32)).astype(BF16)

            @pl.when(j >= 2)
            def _():
                rs_copy(d, j - 2).wait_recv()
                rs_out[d, j] = (mine + sib_in[d, j].astype(F32) + rs_in[d, j - 2].astype(F32)).astype(BF16)

        for d in range(2):
            rs_copy(d, j).start()
        return carry

    for_sibling(0)
    lax.fori_loop(0, items, scatter_step, 0)
    for h in range(2):
        sib_out[h, items] = partial(zeta, 1 - core, h).astype(BF16)
    for h in range(2):
        sp_copy(h, items).start()
    finals = [partial(zeta, core, h) for h in range(2)]
    for h in range(2):
        sp_copy(h, items).wait_recv()
        finals[h] = finals[h] + sib_in[h, items].astype(F32)
    for j in (items - 2, items - 1):
        for d in range(2):
            h = j % 2 if d == 0 else 1 - j % 2
            rs_copy(d, j).wait_recv()
            finals[h] = finals[h] + rs_in[d, j].astype(F32)
    result = jnp.concatenate([f.astype(BF16) for f in finals], axis=0)

    q_row = iota((slots, rows), 0)
    spread = (iota((slots, rows), 1) == q_row - 2 * (q_row >> 3)) & ((q_row & 7) < CAP)
    spread = spread.astype(BF16)
    for c in range(0, width, HD):
        back_out[:, :, c : c + HD] = (
            dot(spread, result[:, c : c + HD]).astype(BF16).reshape(n_exp, PAD, HD)
        )
    back_in[exp] = back_out[exp]

    def bk_copy(k):
        to = lax.rem(exp + k, n_exp)
        return remote(
            back_out.at[to], back_in.at[exp], bk_send.at[k - 1], bk_recv.at[k - 1], {"exp": to}
        )

    def bk_start(k, carry):
        bk_copy(k).start()
        return carry

    def bk_wait(k, carry):
        bk_copy(k).wait_recv()
        return carry

    lax.fori_loop(1, n_exp, bk_start, 0)

    for k in range(n_ff - 1):
        gain_copy(k).wait_send()
    for copy in sig_copies:
        copy.wait_send()
    for h in range(2):
        own_copy(h).wait_send()
        sp_copy(h, items).wait_send()

    def drain(j, carry):
        for d in range(2):
            ag_copy(d, j, zeta, 0).wait_send()
            fwd_copy(d, j, zeta, 0).wait_send()
            sp_copy(d, j).wait_send()
            rs_copy(d, j).wait_send()
        return carry

    lax.fori_loop(0, items, drain, 0)

    def drain_a2a(k, carry):
        a2a_copy(k).wait_send()
        return carry

    lax.fori_loop(1, n_exp, drain_a2a, 0)
    lax.fori_loop(1, n_exp, bk_wait, 0)
    for c in range(0, width, HD):
        picked = dot(sel[...], back_in[:, :, c : c + HD].reshape(slots, HD))
        out_ref[:, c : c + HD] = (stream[:, c : c + HD].astype(F32) + picked).astype(BF16)

    def drain_bk(k, carry):
        bk_copy(k).wait_send()
        return carry

    lax.fori_loop(1, n_exp, drain_bk, 0)


def run_layer(n_exp, n_ff, query, keys, values, residual, gain, logit, ids, wg, wu, wd):
    tokens, width = query.shape
    hidden = wg.shape[1]
    n_ring = 2 * n_ff
    items = n_ring - 1
    rows = n_exp * CAP
    half = rows // 2
    slots = n_exp * PAD
    vmem = pl.BlockSpec(memory_space=pltpu.VMEM)
    hbm = pl.BlockSpec(memory_space=pl.ANY)
    dma = pltpu.SemaphoreType.DMA

    def kernel(*refs):
        layer_kernel(n_exp, n_ff, *refs)

    return pl.pallas_call(
        kernel,
        out_shape=jax.ShapeDtypeStruct((tokens, width), BF16),
        in_specs=[vmem] * 7 + [hbm] * 3,
        out_specs=vmem,
        scratch_shapes=[
            pltpu.VMEM(wg.shape, BF16),
            pltpu.VMEM(wu.shape, BF16),
            pltpu.VMEM(wd.shape, BF16),
            pltpu.VMEM((n_ff, width, 2 * hidden), BF16),
            pltpu.VMEM((tokens, width), BF16),
            pltpu.VMEM((tokens, slots), BF16),
            pltpu.VMEM((n_exp, PAD, width), BF16),
            pltpu.VMEM((n_exp, PAD, width), BF16),
            pltpu.VMEM((n_ff, *gain.shape), F32),
            pltpu.VMEM((4, 2 * n_exp, HD), BF16),
            pltpu.VMEM((n_ring, 2, 2, half, width), BF16),
            pltpu.VMEM((4, 2, half, 2 * hidden), F32),
            pltpu.VMEM((4, 2, half, HD), F32),
            pltpu.VMEM((4, 2, half, hidden), BF16),
            pltpu.VMEM((2, items + 1, half, width), BF16),
            pltpu.VMEM((2, items + 1, half, width), BF16),
            pltpu.VMEM((2, items, half, width), BF16),
            pltpu.VMEM((2, items, half, width), BF16),
            pltpu.VMEM((n_exp, PAD, width), BF16),
            pltpu.VMEM((n_exp, PAD, width), BF16),
            dma((3,)),
            dma((n_ff - 1,)),
            dma((n_ff - 1,)),
            dma((n_exp - 1,)),
            dma((n_exp - 1,)),
            dma((3,)),
            dma((3,)),
            dma((2, items)),
            dma((2, items)),
            dma((2,)),
            dma((2,)),
            dma((2, items)),
            dma((2, items)),
            dma((2, items + 1)),
            dma((2, items + 1)),
            dma((2, items)),
            dma((2, items)),
            dma((n_exp - 1,)),
            dma((n_exp - 1,)),
        ],
        compiler_params=pltpu.CompilerParams(
            collective_id=1, has_side_effects=True, vmem_limit_bytes=60 * 1024 * 1024
        ),
        name="layer",
    )(query, keys, values, residual, gain, logit, ids, wg, wu, wd)


def solution(mesh):
    n_exp, n_ff = mesh.shape["exp"], mesh.shape["ff"]
    torus = Mesh(mesh.devices.reshape(2, 2, n_exp, n_ff), ("zl", "core", "exp", "ff"))

    def body(query, key, value, residual, gain, logit, ids, wg, wu, wd):
        keys, values = gather_kv(key[0], value[0])
        out = run_layer(
            n_exp,
            n_ff,
            query[0],
            keys,
            values,
            residual[0],
            gain.reshape(-1, HD),
            logit,
            ids.reshape(1, -1),
            wg[0],
            wu[0],
            wd[0],
        )
        return out[None]

    placed = (
        P("exp", SEQ, "ff"),
        P("exp", SEQ, "ff"),
        P("exp", SEQ, "ff"),
        P("exp", SEQ, "ff"),
        P("ff"),
        P("exp", SEQ),
        P("exp", SEQ, None),
        P("exp", None, SEQ_FF),
        P("exp", None, SEQ_FF),
        P("exp", SEQ_FF, None),
    )
    return jax.shard_map(
        body, mesh=torus, in_specs=placed, out_specs=P("exp", SEQ, "ff"), check_vma=False
    )
```

time: 285 us -> 96 us (0.34)
  waiting for transfers between devices: 169 us -> 0 us
  Pallas kernels: 0 us -> 94.1 us
  blocking collectives: 68.7 us -> 0 us
  between operations: 13.3 us -> 0.02 us
  matrix products: 12.7 us -> 0 us
  starting transfers between devices: 9.53 us -> 0 us
  local copies, waits for them, and re-layouts: 8.29 us -> 1.6 us
    reduce_scatter x1 -> x0, waiting for transfers between devices: 102 us -> none  [body(): lax.psum_scatter(term.reshape(-1, quarter).astype(jnp.bfloat16), SEQ_FF,...]
    pallas_call x0 -> x2, Pallas kernels: none -> 94.1 us  [the longest x1 85.5 us: run_layer(): pl.pallas_call(kernel, out_shape=jax.ShapeDtypeStruct((tokens, width), BF...]
    all_gather x2 -> x0, waiting for transfers between devices: 60.3 us -> none  [gather_in_order(): parts = lax.all_gather(parts, axes[k])]
    all_to_all x2 -> x0, blocking collectives: 43.1 us -> none  [the longest x1 22.5 us: body(): lax.all_to_all(summed, 'exp', split_axis=0, concat_axis=0, tiled=True)]
    all_gather x2 -> x0, blocking collectives: 25.6 us -> none  [the longest x1 19 us: gather_in_order(): parts = lax.all_gather(parts, axes[k])]
    dot_general x7 -> x0, matrix products: 12.7 us -> none  [the longest x1 8.35 us: body(): jnp.einsum('sjk,kfc->sfjc', activated, down_parts, preferred_element_type...]
    all_to_all x1 -> x0, starting transfers between devices: 9.45 us -> none  [sent_to_all(): return lax.all_to_all(copies, axis, split_axis=0, concat_axis=0, tiled=True)]
    all_to_all x1 -> x0, waiting for transfers between devices: 7.25 us -> none  [sent_to_all(): return lax.all_to_all(copies, axis, split_axis=0, concat_axis=0, tiled=True)]
  transfers between devices with their start and end apart: 4 -> 0, of which waited for: 4 -> 0; matrix products, arithmetic and copies ran while one was open for 1% -> 0% of each run, Pallas kernels for 0% -> 0%
where the time goes in v1:
time: 96 us; the launch traced here: 95.7 us
  Pallas kernels  94.1 us (98%)
  local copies, waits for them, and re-layouts  1.6 us (2%)
    pallas_call x1, Pallas kernels, run_layer(): pl.pallas_call(kernel, out_shape=jax.ShapeDtypeStruct((tokens, width), BF...  85.5 us
    pallas_call x1, Pallas kernels, gather_kv(): pl.pallas_call(kv_kernel, out_shape=(shape, shape), in_specs=[vmem] * 2,...  8.63 us

profile of v1, /device:TPU:6, one launch (start us, length us, event | category | flops | bytes accessed | tf_op | source)
XLA Modules:
  0.0 95.7 jit_solution(13658816784654038945)
XLA Ops:
  0.0 8.6 %gather_kv.1 = (bf16[4,128,128]{2,1,0:T(8,128)(2,1)}, bf16[4,128,128]{2,1,0:T(8,128)(2,1)}) custom-call(bf16[128,128]{1,0:T(8,128)(2,1)} %bitcast.16, bf16[128,128]{1,0:T(8,128)(2,1)} %bitcast.17), custom_call_target="tpu_custom_call" | custom-call | tf_op jit(solution)/shard_map/gather_kv/pallas_call | solution.py:79
  8.6 85.5 %layer.1 = bf16[128,640]{1,0:T(8,128)(2,1)} custom-call(bf16[128,640]{1,0:T(8,128)(2,1)} %bitcast.14, bf16[4,128,128]{2,1,0:T(8,128)(2,1)} %get-tuple-element.7.refs_1_, bf16[4,128,128]{2,1,0:T(8,128)(2,1)} %get-tuple-element.8.refs_2_, bf16[128,640]{1,0:T(8,128)(2,1)} %bitcast.15, f32[5,128]{1,0:T(8,128)} %bitcast.18, f32[1,128]{1,0:T(1,128)} %refs_5_.1, ...), custom_call_target="tpu_custom_call" | custom-call | tf_op jit(solution)/shard_map/layer/pallas_call | solution.py:523
  94.1 1.6 %copy.12 = bf16[1,128,640]{2,1,0:T(8,128)(2,1)} copy(bf16[1,128,640]{2,1,0:T(8,128)(2,1)} %bitcast.13) | data formatting | bytes 327680

commit v2 on v0

v2 whole, which is shorter than its diff:
```python
import jax
import jax.numpy as jnp
from jax import lax
from jax.experimental import pallas as pl
from jax.experimental.pallas import tpu as pltpu
from jax.sharding import Mesh
from jax.sharding import PartitionSpec as P

HD = 128
HEADS = 20
KVH = 4
D = 2560
CAP = 6
ROWS = 16
LOT = 16
LAG = 2
SEQ = ("zl", "core")
SEQ_FF = ("zl", "core", "ff")
NORM_EPS = 1e-05
FLOOR = -1e30
BF16 = jnp.bfloat16
F32 = jnp.float32
MESH = pl.DeviceIdType.MESH


def remote(src, dst, send, recv, where):
    return pltpu.make_async_remote_copy(
        src_ref=src, dst_ref=dst, send_sem=send, recv_sem=recv, device_id=where, device_id_type=MESH
    )


def dot(a, b):
    return jnp.dot(a, b, preferred_element_type=F32)


def dot_rows(a, b):
    return lax.dot_general(a, b, (((0,), (0,)), ((), ())), preferred_element_type=F32)


def dot_cols(a, b):
    return lax.dot_general(a, b, (((1,), (1,)), ((), ())), preferred_element_type=F32)


def iota(shape, dim):
    return lax.broadcasted_iota(jnp.int32, shape, dim)


def as_column(row):
    n = row.shape[-1]
    eye = iota((n, n), 0) == iota((n, n), 1)
    return jnp.sum(jnp.where(eye, jnp.broadcast_to(row, (n, n)), 0.0), axis=1, keepdims=True)


def layer_kernel(
    n_exp,
    n_ff,
    k_hbm,
    v_hbm,
    ids_hbm,
    logit_hbm,
    gain_hbm,
    q_hbm,
    res_hbm,
    wg_hbm,
    wu_hbm,
    wd_hbm,
    out_ref,
    kbuf,
    vbuf,
    ids,
    logit,
    gains,
    query,
    res,
    wg_raw,
    wu_raw,
    wd,
    wgu,
    stream,
    choose,
    owner,
    metas,
    keep,
    widen,
    packed,
    landed,
    sigs,
    xbuf,
    acc,
    sq,
    act,
    sib_out,
    sib_in,
    rs_out,
    rs_in,
    back_out,
    back_in,
    load_sem,
    kv_send,
    kv_recv,
    few_send,
    few_recv,
    a2a_send,
    a2a_recv,
    ring_send,
    ag_recv,
    own_recv,
    fwd_recv,
    sp_recv,
    rs_recv,
    bk_send,
    bk_recv,
):
    n_ring = 2 * n_ff
    items = n_ring - 1
    zl, core = lax.axis_index("zl"), lax.axis_index("core")
    exp, ff = lax.axis_index("exp"), lax.axis_index("ff")
    shard = zl * 2 + core
    zeta = ff * 2 + zl
    tokens, width = query.shape
    cols = width // HD
    part = CAP // 2
    half = n_exp * part
    hidden = wg_raw.shape[1]
    lot = min(n_exp, LOT)

    def at_ring(step):
        z = lax.rem(zeta + step + n_ring, n_ring)
        return {"zl": lax.rem(z, 2), "ff": z // 2}

    sibling = {"core": 1 - core}
    seq_peers = ({"zl": 1 - zl, "core": 1 - core}, {"zl": 1 - zl}, sibling)
    nxt = (at_ring(1), at_ring(-1))
    ff_peers = [{"ff": lax.rem(ff + k, n_ff)} for k in range(1, n_ff)]

    loads = [
        pltpu.make_async_copy(src, dst, load_sem.at[n])
        for n, (src, dst) in enumerate(
            (
                (ids_hbm, ids),
                (logit_hbm, logit),
                (k_hbm, kbuf.at[shard]),
                (v_hbm, vbuf.at[shard]),
                (gain_hbm, gains.at[ff]),
                (q_hbm, query),
                (res_hbm, res),
                (wg_hbm, wg_raw),
                (wu_hbm, wu_raw),
                (wd_hbm, wd),
            )
        )
    ]
    for load in loads:
        load.start()
    barrier = pltpu.get_barrier_semaphore()
    greeted = [sibling, {"zl": 1 - zl, "core": 1 - core}, *nxt]
    for where in greeted + ff_peers:
        pl.semaphore_signal(barrier, inc=1, device_id=where, device_id_type=MESH)

    def greet(k, carry):
        pl.semaphore_signal(
            barrier, inc=1, device_id={"exp": lax.rem(exp + k, n_exp)}, device_id_type=MESH
        )
        return carry

    lax.fori_loop(1, n_exp, greet, 0)
    loads[2].wait()
    loads[3].wait()
    loads[4].wait()

    pl.semaphore_wait(barrier, n_exp - 1 + len(greeted) + len(ff_peers))
    for n, buf in enumerate((kbuf, vbuf)):
        for where in seq_peers:
            remote(buf.at[shard], buf.at[shard], kv_send.at[n], kv_recv.at[n], where).start()
    for where in ff_peers:
        remote(gains.at[ff], gains.at[ff], few_send.at[0], few_recv.at[0], where).start()

    loads[0].wait()
    loads[1].wait()
    route = ids[...]
    onehot = (jnp.broadcast_to(route, (HD, tokens)) == iota((HD, tokens), 0)).astype(F32)
    below = (iota((tokens, tokens), 0) < iota((tokens, tokens), 1)).astype(BF16)
    earlier = dot(onehot.astype(BF16), below)
    slot = jnp.sum(earlier * onehot, axis=0, keepdims=True).astype(jnp.int32)
    gate_in = as_column(jax.nn.sigmoid(logit[...]))
    gate_hi = gate_in.astype(BF16).astype(F32)
    gate_lo = gate_in - gate_hi
    lane = iota((tokens, HD), 1)
    for h in range(2):
        mine = (slot >= part * h) & (slot < part * (h + 1))
        target = jnp.where(mine, route * part + slot - part * h, -1)
        choose[h] = (iota((half, tokens), 0) == target).astype(BF16)
        expert = jnp.where(mine, route, -1)
        owner[h] = (iota((n_exp, tokens), 0) == expert).astype(BF16)
        place = as_column((slot - part * h).astype(F32)).astype(jnp.int32)
        metas[h] = jnp.where(
            lane == place, gate_hi, jnp.where(lane == place + HD // 2, gate_lo, 0.0)
        ).astype(BF16)

    def dense_row(r):
        in_block = r & (ROWS - 1)
        b = (in_block * 11) >> 5
        row = b * (lot * part) + (r >> 4) * part + in_block - part * b
        return jnp.where(in_block < ROWS - 1, row, cols * lot * part + (r >> 4))

    lot_rows = lot * ROWS
    dense_rows = (cols * part + 1) * lot
    keep[...] = (
        iota((dense_rows, lot_rows), 0) == dense_row(iota((dense_rows, lot_rows), 1))
    ).astype(BF16)
    widen[...] = (
        iota((lot_rows, dense_rows), 1) == dense_row(iota((lot_rows, dense_rows), 0))
    ).astype(BF16)
    acc[...] = jnp.zeros_like(acc)
    sq[...] = jnp.zeros_like(sq)

    def to_blocks(target, h, dense, extra):
        for n in range(0, n_exp, lot):
            stack = [dense[n * part : (n + lot) * part, b * HD : (b + 1) * HD] for b in range(cols)]
            stack = jnp.concatenate(stack + [extra[n : n + lot]], axis=0)
            block = dot(widen[...], stack).astype(BF16)
            target[h, n : n + lot] = block.reshape(lot, ROWS, HD)

    def from_blocks(source, h, n):
        return dot(keep[...], source[h, n : n + lot].reshape(lot_rows, HD)).astype(BF16)

    loads[5].wait()
    loads[6].wait()

    span = 4 * tokens
    group = HEADS // KVH
    pltpu.make_async_copy(kbuf.at[0:3], kbuf.at[0:3], kv_recv.at[0]).wait()
    pltpu.make_async_copy(vbuf.at[0:3], vbuf.at[0:3], kv_recv.at[1]).wait()
    allowed = iota((tokens, span), 1) <= iota((tokens, span), 0) + shard * tokens
    for a in range(kbuf.shape[2] // HD):
        keys = kbuf[:, :, a * HD : (a + 1) * HD].reshape(span, HD)
        values = vbuf[:, :, a * HD : (a + 1) * HD].reshape(span, HD)
        for g in range(group):
            h = (a * group + g) * HD
            scores = dot_cols(query[:, h : h + HD], keys) * HD ** (-0.5)
            scores = jnp.where(allowed, scores, FLOOR)
            peak = jnp.max(scores, axis=-1, keepdims=True)
            weights = jnp.where(allowed, jnp.exp(scores - peak), 0.0)
            total = jnp.sum(weights, axis=-1, keepdims=True)
            mixed = dot(weights.astype(BF16), values) / total
            stream[:, h : h + HD] = (res[:, h : h + HD].astype(F32) + mixed).astype(BF16)

    def a2a_copy(h, k):
        to = lax.rem(exp + k, n_exp)
        return remote(packed.at[h, to], landed.at[h, exp], a2a_send.at[h], a2a_recv.at[h], {"exp": to})

    for h in range(2):
        dense = dot(choose[h], stream[...]).astype(BF16)
        to_blocks(packed, h, dense, dot(owner[h], metas[h]).astype(BF16))
        landed[h, exp] = packed[h, exp]

        def a2a_start(k, carry):
            a2a_copy(h, k).start()
            return carry

        lax.fori_loop(1, n_exp, a2a_start, 0)

    for n in range(7, 10):
        loads[n].wait()
    pltpu.make_async_copy(gains.at[0 : n_ff - 1], gains.at[0 : n_ff - 1], few_recv.at[0]).wait()

    def fold(b, carry):
        f = b // cols
        r = b - f * cols
        column = as_column(gains[f, pl.ds(r, 1), :])
        src = pl.ds(pl.multiple_of(b * HD, HD), HD)
        dst = pl.ds(pl.multiple_of(r * HD, HD), HD)
        wgu[f, dst, 0:hidden] = (wg_raw[src, :].astype(F32) * column).astype(BF16)
        wgu[f, dst, hidden : 2 * hidden] = (wu_raw[src, :].astype(F32) * column).astype(BF16)
        return carry

    lax.fori_loop(0, n_ff * cols, fold, 0)
    def a2a_landed(h):
        some = pl.ds(0, n_exp - 1)
        pltpu.make_async_copy(packed.at[h, some], landed.at[h, some], a2a_recv.at[h]).wait()

    def own_dense(h):
        with jax.named_scope(f"land#h={h}"):
            a2a_landed(h)
        for n in range(0, n_exp, lot):
            dense = from_blocks(landed, h, n)
            for b in range(cols):
                xbuf[zeta, core, h, n * part : (n + lot) * part, b * HD : (b + 1) * HD] = dense[
                    b * lot * part : (b + 1) * lot * part
                ]
            sigs[shard, h, n : n + lot] = dense[cols * lot * part :]

    quarter = half // 2

    def quarter_of(v):
        return pl.ds(v * quarter, quarter)

    def ring_item(d, p):
        k = p // 2 + 1
        z = lax.rem((zeta - k if d == 0 else zeta + k) + n_ring, n_ring)
        h = lax.rem(p, 2)
        return z, (h if d == 0 else jnp.where(p == items - 1, 1, h))

    def ag_copy(d, p, v, z, h):
        ref = xbuf.at[z, core, h, quarter_of(v)]
        return remote(ref, ref, ring_send.at[0], ag_recv.at[d, p, v], nxt[d])

    def own_copy(c, h):
        ref = xbuf.at[zeta, c, h]
        return remote(ref, ref, ring_send.at[1], own_recv.at[h], sibling)

    def fwd_copy(d, p, z, c, h):
        ref = xbuf.at[z, c, h]
        return remote(ref, ref, ring_send.at[2], fwd_recv.at[d, p], sibling)

    def multiply(z, c, h):
        x = xbuf[z, c, h]
        s = lax.rem(z, 2) * 2 + c
        acc[s, h] += dot(x, wgu[z // 2])
        squares = None
        for b in range(cols):
            xf = x[:, b * HD : (b + 1) * HD].astype(F32)
            squares = xf * xf if squares is None else squares + xf * xf
        sq[s, h] += squares

    for h in range(2):
        own_dense(h)
        own_copy(core, h).start()
        for v in range(2):
            for d in range(2):
                ag_copy(d, h, v, zeta, h).start()
        if h == 0:
            multiply(zeta, core, h)

    for where in seq_peers:
        remote(sigs.at[shard], sigs.at[shard], few_send.at[1], few_recv.at[1], where).start()

    multiply(zeta, core, 1)

    def from_sibling(p):
        for d in range(2):
            z, h = ring_item(d, p)
            fwd_copy(d, p, z, 1 - core, h).wait_recv()
            multiply(z, 1 - core, h)

    def gather_step(p, carry):
        for v in range(2):
            for d in range(2):
                z, h = ring_item(d, p)
                with jax.named_scope(f"arrive#v={v}#d={d}"):
                    ag_copy(d, p, v, z, h).wait_recv()
                if d == 0:

                    @pl.when(p < items - 2)
                    def _():
                        ag_copy(d, p + 2, v, z, h).start()

                else:

                    @pl.when(p < items - 3)
                    def _():
                        ag_copy(d, p + 2, v, z, h).start()

                    @pl.when(p == items - 2)
                    def _():
                        ag_copy(d, p + 1, v, z, h).start()

        for d in range(2):
            z, h = ring_item(d, p)
            fwd_copy(d, p, z, core, h).start()
        for d in range(2):
            z, h = ring_item(d, p)
            multiply(z, core, h)

        @pl.when(p >= LAG)
        def _():
            from_sibling(p - LAG)

        return carry

    lax.fori_loop(0, LAG, gather_step, 0)
    for h in range(2):
        own_copy(1 - core, h).wait_recv()
        multiply(zeta, 1 - core, h)
    lax.fori_loop(LAG, items, gather_step, 0)
    for p in range(items - LAG, items):
        from_sibling(p)

    pltpu.make_async_copy(sigs.at[0:3], sigs.at[0:3], few_recv.at[1]).wait()
    first = part * iota((half, n_exp), 1)
    spread = (iota((half, n_exp), 0) >= first) & (iota((half, n_exp), 0) < first + part)
    spread = spread.astype(BF16)
    r_lane = iota((half, HD), 0)
    here = (r_lane - part * ((r_lane * 171) >> 9)) == (iota((half, HD), 1) & (HD // 2 - 1))
    for h in range(2):
        for s in range(4):
            sig = jnp.sum(jnp.where(here, dot(spread, sigs[s, h]), 0.0), axis=1, keepdims=True)
            meansq = jnp.sum(sq[s, h], axis=1, keepdims=True) / D
            factor = lax.rsqrt(meansq + NORM_EPS) * sig
            gate = acc[s, h, :, 0:hidden] * factor
            up = acc[s, h, :, hidden : 2 * hidden] * factor
            act[s, h] = (gate / (1.0 + jnp.exp(-gate)) * up).astype(BF16)

    def partial(z, c, h):
        s = lax.rem(z, 2) * 2 + c
        return dot(act[s, h], wd[:, pl.ds(pl.multiple_of((z // 2) * width, HD), width)])

    def rs_target(d, p):
        k = n_ff - (p + 1) // 2
        z = lax.rem((zeta + k if d == 0 else zeta - k) + n_ring, n_ring)
        h = lax.rem(p + 1, 2)
        return z, (jnp.where(p == 0, 0, h) if d == 0 else h)

    def sp_copy(d, p):
        return remote(sib_out.at[d, p], sib_in.at[d, p], ring_send.at[3], sp_recv.at[d, p], sibling)

    def for_sibling(p):
        for d in range(2):
            z, h = rs_target(d, p)
            sib_out[d, p] = partial(z, 1 - core, h).astype(BF16)
        for d in range(2):
            sp_copy(d, p).start()

    def rs_copy(d, p, v):
        return remote(
            rs_out.at[d, p, quarter_of(v)],
            rs_in.at[d, p, quarter_of(v)],
            ring_send.at[4],
            rs_recv.at[d, p, v],
            nxt[d],
        )

    def scatter_step(p, before):
        mine = []
        for d in range(2):
            z, h = rs_target(d, p)
            own = partial(z, core, h)
            sp_copy(d, p).wait_recv()
            mine.append(own + sib_in[d, p].astype(F32))
        for v in range(2):
            rows = quarter_of(v)
            for d in range(2):
                block = mine[d][v * quarter : (v + 1) * quarter]
                if before[d] is not None:
                    rs_copy(d, before[d], v).wait_recv()
                    block = block + rs_in[d, before[d], rows].astype(F32)
                rs_out[d, p, rows] = block.astype(BF16)
            for d in range(2):
                rs_copy(d, p, v).start()

    def chained_step(p, carry):
        scatter_step(p, (p - 2, p - 2))
        return carry

    for_sibling(0)
    for_sibling(1)
    scatter_step(0, (None, None))
    for_sibling(2)
    for_sibling(3)
    scatter_step(1, (0, None))
    for_sibling(4)
    for_sibling(5)
    scatter_step(2, (None, 0))
    for_sibling(6)
    for h in range(2):
        sib_out[h, items] = partial(zeta, 1 - core, h).astype(BF16)
    for h in range(2):
        sp_copy(h, items).start()
    lax.fori_loop(3, items, chained_step, 0)

    def bk_copy(h, k):
        to = lax.rem(exp + k, n_exp)
        return remote(back_out.at[h, to], back_in.at[h, exp], bk_send.at[h], bk_recv.at[h], {"exp": to})

    finals = [partial(zeta, core, h) for h in range(2)]
    for h in range(2):
        sp_copy(h, items).wait_recv()
        finals[h] = finals[h] + sib_in[h, items].astype(F32)
    blank = jnp.zeros((n_exp, HD), BF16)
    for h in range(2):
        p = items - 2 + h
        for d in range(2):
            for v in range(2):
                rs_copy(d, p, v).wait_recv()
        dense = finals[h] + rs_in[0, p].astype(F32) + rs_in[1, p].astype(F32)
        to_blocks(back_out, h, dense.astype(BF16), blank)
        back_in[h, exp] = back_out[h, exp]

        def bk_start(k, carry):
            bk_copy(h, k).start()
            return carry

        lax.fori_loop(1, n_exp, bk_start, 0)

    def sent(ref, sem):
        pltpu.make_async_copy(ref, ref, sem).wait()

    for n, buf in enumerate((kbuf, vbuf)):
        sent(buf.at[0:3], kv_send.at[n])
    sent(gains.at[0 : n_ff - 1], few_send.at[0])
    sent(sigs.at[0:3], few_send.at[1])
    for n in (0, 2, 4):
        sent(rs_out, ring_send.at[n])
    sent(xbuf.at[0, 0], ring_send.at[1])
    sent(sib_out, ring_send.at[3])
    for h in range(2):
        sent(packed.at[h, pl.ds(0, n_exp - 1)], a2a_send.at[h])

    total = None
    for h in range(2):
        some = pl.ds(0, n_exp - 1)
        pltpu.make_async_copy(back_out.at[h, some], back_in.at[h, some], bk_recv.at[h]).wait()
        lots = [from_blocks(back_in, h, n) for n in range(0, n_exp, lot)]
        step = lot * part
        dense = [
            jnp.concatenate([x[b * step : (b + 1) * step] for x in lots], axis=0) for b in range(cols)
        ]
        picked = dot_rows(choose[h], jnp.concatenate(dense, axis=1))
        total = picked if total is None else total + picked

    out_ref[...] = (stream[...].astype(F32) + total).astype(BF16)
    for h in range(2):
        sent(back_out.at[h, pl.ds(0, n_exp - 1)], bk_send.at[h])


def run_layer(n_exp, n_ff, key, value, ids, logit, gain, query, residual, wg, wu, wd):
    tokens, width = query.shape
    hidden = wg.shape[1]
    items = 2 * n_ff - 1
    cols = width // HD
    half = n_exp * CAP // 2
    lot_rows = min(n_exp, LOT) * ROWS
    dense_rows = (cols * CAP // 2 + 1) * min(n_exp, LOT)
    dma = pltpu.SemaphoreType.DMA

    def kernel(*refs):
        layer_kernel(n_exp, n_ff, *refs)

    def like(x):
        return pltpu.VMEM(x.shape, x.dtype)

    blocks = pltpu.VMEM((2, n_exp, ROWS, HD), BF16)
    return pl.pallas_call(
        kernel,
        out_shape=pltpu.VMEM((tokens, width), BF16),
        in_specs=[pl.BlockSpec(memory_space=pl.ANY)] * 10,
        out_specs=pl.BlockSpec(memory_space=pltpu.VMEM),
        scratch_shapes=[
            pltpu.VMEM((4, *key.shape), BF16),
            pltpu.VMEM((4, *value.shape), BF16),
            like(ids),
            like(logit),
            pltpu.VMEM((n_ff, *gain.shape), F32),
            like(query),
            like(residual),
            like(wg),
            like(wu),
            like(wd),
            pltpu.VMEM((n_ff, width, 2 * hidden), BF16),
            pltpu.VMEM((tokens, width), BF16),
            pltpu.VMEM((2, half, tokens), BF16),
            pltpu.VMEM((2, n_exp, tokens), BF16),
            pltpu.VMEM((2, tokens, HD), BF16),
            pltpu.VMEM((dense_rows, lot_rows), BF16),
            pltpu.VMEM((lot_rows, dense_rows), BF16),
            blocks,
            blocks,
            pltpu.VMEM((4, 2, n_exp, HD), BF16),
            pltpu.VMEM((2 * n_ff, 2, 2, half, width), BF16),
            pltpu.VMEM((4, 2, half, 2 * hidden), F32),
            pltpu.VMEM((4, 2, half, HD), F32),
            pltpu.VMEM((4, 2, half, hidden), BF16),
            pltpu.VMEM((2, items + 1, half, width), BF16),
            pltpu.VMEM((2, items + 1, half, width), BF16),
            pltpu.VMEM((2, items, half, width), BF16),
            pltpu.VMEM((2, items, half, width), BF16),
            blocks,
            blocks,
            dma((10,)),
            dma((2,)),
            dma((2,)),
            dma((2,)),
            dma((2,)),
            dma((2,)),
            dma((2,)),
            dma((5,)),
            dma((2, items, 2)),
            dma((2,)),
            dma((2, items)),
            dma((2, items + 1)),
            dma((2, items, 2)),
            dma((2,)),
            dma((2,)),
        ],
        compiler_params=pltpu.CompilerParams(
            collective_id=0, has_side_effects=True, vmem_limit_bytes=60 * 1024 * 1024
        ),
        name="layer",
    )(key, value, ids, logit, gain, query, residual, wg, wu, wd)


def solution(mesh):
    n_exp, n_ff = mesh.shape["exp"], mesh.shape["ff"]
    torus = Mesh(mesh.devices.reshape(2, 2, n_exp, n_ff), ("zl", "core", "exp", "ff"))

    def body(query, key, value, residual, gain, logit, ids, wg, wu, wd):
        out = run_layer(
            n_exp,
            n_ff,
            key[0],
            value[0],
            ids.reshape(1, -1),
            logit,
            gain.reshape(-1, HD),
            query[0],
            residual[0],
            wg[0],
            wu[0],
            wd[0],
        )
        return out[None]

    placed = (
        P("exp", SEQ, "ff"),
        P("exp", SEQ, "ff"),
        P("exp", SEQ, "ff"),
        P("exp", SEQ, "ff"),
        P("ff"),
        P("exp", SEQ),
        P("exp", SEQ, None),
        P("exp", None, SEQ_FF),
        P("exp", None, SEQ_FF),
        P("exp", SEQ_FF, None),
    )
    return jax.shard_map(
        body, mesh=torus, in_specs=placed, out_specs=P("exp", SEQ, "ff"), check_vma=False
    )
```

time: 285 us -> 87.3 us (0.31)
  waiting for transfers between devices: 169 us -> 0 us
  Pallas kernels: 0 us -> 85.5 us
  blocking collectives: 68.7 us -> 0 us
  between operations: 13.3 us -> 0.01 us
  matrix products: 12.7 us -> 0 us
  starting transfers between devices: 9.53 us -> 0 us
  local copies, waits for them, and re-layouts: 8.29 us -> 0.67 us
    reduce_scatter x1 -> x0, waiting for transfers between devices: 102 us -> none  [body(): lax.psum_scatter(term.reshape(-1, quarter).astype(jnp.bfloat16), SEQ_FF,...]
    pallas_call x0 -> x1, Pallas kernels: none -> 85.5 us  [run_layer(): pl.pallas_call(kernel, out_shape=pltpu.VMEM((tokens, width), BF16), in_sp...]
    all_gather x2 -> x0, waiting for transfers between devices: 60.3 us -> none  [gather_in_order(): parts = lax.all_gather(parts, axes[k])]
    all_to_all x2 -> x0, blocking collectives: 43.1 us -> none  [the longest x1 22.5 us: body(): lax.all_to_all(summed, 'exp', split_axis=0, concat_axis=0, tiled=True)]
    all_gather x2 -> x0, blocking collectives: 25.6 us -> none  [the longest x1 19 us: gather_in_order(): parts = lax.all_gather(parts, axes[k])]
    dot_general x7 -> x0, matrix products: 12.7 us -> none  [the longest x1 8.35 us: body(): jnp.einsum('sjk,kfc->sfjc', activated, down_parts, preferred_element_type...]
    all_to_all x1 -> x0, starting transfers between devices: 9.45 us -> none  [sent_to_all(): return lax.all_to_all(copies, axis, split_axis=0, concat_axis=0, tiled=True)]
    all_to_all x1 -> x0, waiting for transfers between devices: 7.25 us -> none  [sent_to_all(): return lax.all_to_all(copies, axis, split_axis=0, concat_axis=0, tiled=True)]
  transfers between devices with their start and end apart: 4 -> 0, of which waited for: 4 -> 0; matrix products, arithmetic and copies ran while one was open for 1% -> 0% of each run, Pallas kernels for 0% -> 0%
where the time goes in v2:
time: 87.3 us; the launch traced here: 86.2 us
  Pallas kernels  85.5 us (98%)
    pallas_call x1, Pallas kernels, run_layer(): pl.pallas_call(kernel, out_shape=pltpu.VMEM((tokens, width), BF16), in_sp...  85.5 us

profile of v2, /device:TPU:6, one launch (start us, length us, event | category | flops | bytes accessed | tf_op | source)
XLA Modules:
  0.0 86.2 jit_solution(6862746962264200749)
XLA Ops:
  0.0 85.5 %layer.1 = bf16[128,640]{1,0:T(8,128)(2,1)S(1)} custom-call(bf16[128,128]{1,0:T(8,128)(2,1)} %bitcast.16, bf16[128,128]{1,0:T(8,128)(2,1)} %bitcast.17, s32[1,128]{1,0:T(1,128)} %bitcast.19, f32[1,128]{1,0:T(1,128)} %refs_3_.1, f32[5,128]{1,0:T(8,128)} %bitcast.18, bf16[128,640]{1,0:T(8,128)(2,1)} %bitcast.14, bf16[128,640]{1,0:T(8,128)(2,1)} %bitcast.15, ...), custom_call_target="tpu_custom_call" | custom-call | tf_op jit(solution)/shard_map/layer/pallas_call | solution.py:543
  85.5 0.7 copy.12

commit v3 on v2

--- a/solution.py
+++ b/solution.py
@@ -23,6 +23,30 @@
 MESH = pl.DeviceIdType.MESH
 
 
+AG_ORDER = (
+    [(p, v) for p in range(7) for v in range(2)],
+    [(p, v) for p in range(4) for v in range(2)] + [(4, 0), (5, 0), (5, 1), (4, 1), (6, 0), (6, 1)],
+)
+AG_ONWARD = (
+    {(p, v): ((p, v, p + 2),) for p in range(5) for v in range(2)},
+    {
+        **{(p, v): ((p, v, p + 2),) for p in range(2) for v in range(2)},
+        (2, 0): ((2, 0, 4),),
+        (3, 0): ((3, 0, 5),),
+        (3, 1): ((3, 1, 5), (2, 1, 4)),
+        (5, 0): ((5, 0, 6),),
+        (5, 1): ((5, 1, 6),),
+    },
+)
+AG_WHOLE = [[(0, p), (1, p)] for p in range(4)] + [[(0, 4)], [(0, 5), (1, 5), (1, 4)], [(0, 6), (1, 6)]]
+RS_ORDER = (
+    [(2, 0), (2, 1), (0, 0), (0, 1), (4, 0), (1, 0), (1, 1), (4, 1), (3, 0), (3, 1), (6, 0), (5, 0), (5, 1), (6, 1)],
+    [(1, 0), (1, 1), (0, 0), (0, 1), (3, 0), (2, 0), (2, 1), (3, 1), (4, 0), (4, 1), (5, 0), (5, 1), (6, 0), (6, 1)],
+)
+RS_BEFORE = ({1: 0, 3: 1, 5: 3, 4: 2, 6: 4}, {2: 0, 4: 2, 6: 4, 3: 1, 5: 3})
+RS_GROUPS = ((2, 1), (0, 0), (4, 3), (1, 2), (3, 4), (6, 5), (5, 6))
+
+
 def remote(src, dst, send, recv, where):
     return pltpu.make_async_remote_copy(
         src_ref=src, dst_ref=dst, send_sem=send, recv_sem=recv, device_id=where, device_id_type=MESH
@@ -49,6 +73,13 @@
     n = row.shape[-1]
     eye = iota((n, n), 0) == iota((n, n), 1)
     return jnp.sum(jnp.where(eye, jnp.broadcast_to(row, (n, n)), 0.0), axis=1, keepdims=True)
+
+
+def far_first(n_exp):
+    ny = min(n_exp, 8)
+    nx = n_exp // ny
+    offsets = [(dx, dy) for dx in range(nx) for dy in range(ny) if dx or dy]
+    return sorted(offsets, key=lambda o: -(min(o[0], nx - o[0]) + min(o[1], ny - o[1]))), nx, ny
 
 
 def layer_kernel(
@@ -93,6 +124,7 @@
     sib_in,
     rs_out,
     rs_in,
+    mine,
     back_out,
     back_in,
     load_sem,
@@ -133,6 +165,13 @@
     nxt = (at_ring(1), at_ring(-1))
     ff_peers = [{"ff": lax.rem(ff + k, n_ff)} for k in range(1, n_ff)]
 
+    offsets, nx, ny = far_first(n_exp)
+    exp_x, exp_y = exp // ny, lax.rem(exp, ny)
+
+    def partner(offset):
+        dx, dy = offset
+        return lax.rem(exp_x + dx, nx) * ny + lax.rem(exp_y + dy, ny)
+
     loads = [
         pltpu.make_async_copy(src, dst, load_sem.at[n])
         for n, (src, dst) in enumerate(
@@ -157,13 +196,10 @@
     for where in greeted + ff_peers:
         pl.semaphore_signal(barrier, inc=1, device_id=where, device_id_type=MESH)
 
-    def greet(k, carry):
+    for offset in offsets:
         pl.semaphore_signal(
-            barrier, inc=1, device_id={"exp": lax.rem(exp + k, n_exp)}, device_id_type=MESH
+            barrier, inc=1, device_id={"exp": partner(offset)}, device_id_type=MESH
         )
-        return carry
-
-    lax.fori_loop(1, n_exp, greet, 0)
     loads[2].wait()
     loads[3].wait()
     loads[4].wait()
@@ -187,10 +223,10 @@
     gate_lo = gate_in - gate_hi
     lane = iota((tokens, HD), 1)
     for h in range(2):
-        mine = (slot >= part * h) & (slot < part * (h + 1))
-        target = jnp.where(mine, route * part + slot - part * h, -1)
+        inside = (slot >= part * h) & (slot < part * (h + 1))
+        target = jnp.where(inside, route * part + slot - part * h, -1)
         choose[h] = (iota((half, tokens), 0) == target).astype(BF16)
-        expert = jnp.where(mine, route, -1)
+        expert = jnp.where(inside, route, -1)
         owner[h] = (iota((n_exp, tokens), 0) == expert).astype(BF16)
         place = as_column((slot - part * h).astype(F32)).astype(jnp.int32)
         metas[h] = jnp.where(
@@ -245,20 +281,25 @@
             mixed = dot(weights.astype(BF16), values) / total
             stream[:, h : h + HD] = (res[:, h : h + HD].astype(F32) + mixed).astype(BF16)
 
-    def a2a_copy(h, k):
-        to = lax.rem(exp + k, n_exp)
+    def a2a_copy(h, offset):
+        to = partner(offset)
         return remote(packed.at[h, to], landed.at[h, exp], a2a_send.at[h], a2a_recv.at[h], {"exp": to})
 
-    for h in range(2):
-        dense = dot(choose[h], stream[...]).astype(BF16)
-        to_blocks(packed, h, dense, dot(owner[h], metas[h]).astype(BF16))
+    dense = dot(choose[...].reshape(2 * half, tokens), stream[...]).astype(BF16)
+    extra = [dot(owner[h], metas[h]).astype(BF16) for h in range(2)]
+    for n in range(0, n_exp, lot):
+        sides = []
+        for h in range(2):
+            at = h * half + n * part
+            stack = [dense[at : at + lot * part, b * HD : (b + 1) * HD] for b in range(cols)]
+            sides.append(jnp.concatenate(stack + [extra[h][n : n + lot]], axis=0))
+        block = dot(widen[...], jnp.concatenate(sides, axis=1)).astype(BF16)
+        for h in range(2):
+            packed[h, n : n + lot] = block[:, h * HD : (h + 1) * HD].reshape(lot, ROWS, HD)
+    for h in range(2):
         landed[h, exp] = packed[h, exp]
-
-        def a2a_start(k, carry):
-            a2a_copy(h, k).start()
-            return carry
-
-        lax.fori_loop(1, n_exp, a2a_start, 0)
+        for offset in offsets:
+            a2a_copy(h, offset).start()
 
     for n in range(7, 10):
         loads[n].wait()
@@ -298,8 +339,7 @@
     def ring_item(d, p):
         k = p // 2 + 1
         z = lax.rem((zeta - k if d == 0 else zeta + k) + n_ring, n_ring)
-        h = lax.rem(p, 2)
-        return z, (h if d == 0 else jnp.where(p == items - 1, 1, h))
+        return z, (1 if d == 1 and p == items - 1 else p % 2)
 
     def ag_copy(d, p, v, z, h):
         ref = xbuf.at[z, core, h, quarter_of(v)]
@@ -337,54 +377,42 @@
 
     multiply(zeta, core, 1)
 
-    def from_sibling(p):
-        for d in range(2):
-            z, h = ring_item(d, p)
-            fwd_copy(d, p, z, 1 - core, h).wait_recv()
-            multiply(z, 1 - core, h)
-
-    def gather_step(p, carry):
-        for v in range(2):
+    def from_sibling(d, p):
+        z, h = ring_item(d, p)
+        fwd_copy(d, p, z, 1 - core, h).wait_recv()
+        multiply(z, 1 - core, h)
+
+    def onward(d, p, v, to):
+        z, h = ring_item(d, p)
+        ag_copy(d, to, v, z, h).start()
+
+    def take(slot):
+        for n in (2 * slot, 2 * slot + 1):
             for d in range(2):
+                p, v = AG_ORDER[d][n]
                 z, h = ring_item(d, p)
-                with jax.named_scope(f"arrive#v={v}#d={d}"):
-                    ag_copy(d, p, v, z, h).wait_recv()
-                if d == 0:
-
-                    @pl.when(p < items - 2)
-                    def _():
-                        ag_copy(d, p + 2, v, z, h).start()
-
-                else:
-
-                    @pl.when(p < items - 3)
-                    def _():
-                        ag_copy(d, p + 2, v, z, h).start()
-
-                    @pl.when(p == items - 2)
-                    def _():
-                        ag_copy(d, p + 1, v, z, h).start()
-
-        for d in range(2):
+                ag_copy(d, p, v, z, h).wait_recv()
+                for p_on, v_on, to in AG_ONWARD[d].get((p, v), ()):
+                    onward(d, p_on, v_on, to)
+        for d, p in AG_WHOLE[slot]:
             z, h = ring_item(d, p)
             fwd_copy(d, p, z, core, h).start()
-        for d in range(2):
+        for d, p in AG_WHOLE[slot]:
             z, h = ring_item(d, p)
             multiply(z, core, h)
 
-        @pl.when(p >= LAG)
-        def _():
-            from_sibling(p - LAG)
-
-        return carry
-
-    lax.fori_loop(0, LAG, gather_step, 0)
-    for h in range(2):
-        own_copy(1 - core, h).wait_recv()
-        multiply(zeta, 1 - core, h)
-    lax.fori_loop(LAG, items, gather_step, 0)
-    for p in range(items - LAG, items):
-        from_sibling(p)
+    for slot in range(items - 1):
+        take(slot)
+        if slot == 1:
+            for h in range(2):
+                own_copy(1 - core, h).wait_recv()
+                multiply(zeta, 1 - core, h)
+        if slot >= LAG:
+            for d, p in AG_WHOLE[slot - LAG]:
+                from_sibling(d, p)
+    for slot in range(items - 1 - LAG, items - 1):
+        for d, p in AG_WHOLE[slot]:
+            from_sibling(d, p)
 
     pltpu.make_async_copy(sigs.at[0:3], sigs.at[0:3], few_recv.at[1]).wait()
     first = part * iota((half, n_exp), 1)
@@ -392,14 +420,17 @@
     spread = spread.astype(BF16)
     r_lane = iota((half, HD), 0)
     here = (r_lane - part * ((r_lane * 171) >> 9)) == (iota((half, HD), 1) & (HD // 2 - 1))
-    for h in range(2):
-        for s in range(4):
-            sig = jnp.sum(jnp.where(here, dot(spread, sigs[s, h]), 0.0), axis=1, keepdims=True)
-            meansq = jnp.sum(sq[s, h], axis=1, keepdims=True) / D
-            factor = lax.rsqrt(meansq + NORM_EPS) * sig
-            gate = acc[s, h, :, 0:hidden] * factor
-            up = acc[s, h, :, hidden : 2 * hidden] * factor
-            act[s, h] = (gate / (1.0 + jnp.exp(-gate)) * up).astype(BF16)
+
+    def activate(z_part):
+        for c in range(2):
+            s = z_part * 2 + c
+            for h in range(2):
+                sig = jnp.sum(jnp.where(here, dot(spread, sigs[s, h]), 0.0), axis=1, keepdims=True)
+                meansq = jnp.sum(sq[s, h], axis=1, keepdims=True) / D
+                factor = lax.rsqrt(meansq + NORM_EPS) * sig
+                gate = acc[s, h, :, 0:hidden] * factor
+                up = acc[s, h, :, hidden : 2 * hidden] * factor
+                act[s, h] = (gate / (1.0 + jnp.exp(-gate)) * up).astype(BF16)
 
     def partial(z, c, h):
         s = lax.rem(z, 2) * 2 + c
@@ -408,18 +439,25 @@
     def rs_target(d, p):
         k = n_ff - (p + 1) // 2
         z = lax.rem((zeta + k if d == 0 else zeta - k) + n_ring, n_ring)
-        h = lax.rem(p + 1, 2)
-        return z, (jnp.where(p == 0, 0, h) if d == 0 else h)
+        return z, (0 if d == 0 and p == 0 else (p + 1) % 2)
 
     def sp_copy(d, p):
         return remote(sib_out.at[d, p], sib_in.at[d, p], ring_send.at[3], sp_recv.at[d, p], sibling)
 
-    def for_sibling(p):
+    def for_sibling(group):
         for d in range(2):
+            z, h = rs_target(d, RS_GROUPS[group][d])
+            sib_out[d, RS_GROUPS[group][d]] = partial(z, 1 - core, h).astype(BF16)
+        for d in range(2):
+            sp_copy(d, RS_GROUPS[group][d]).start()
+
+    def prepare(group):
+        for d in range(2):
+            p = RS_GROUPS[group][d]
             z, h = rs_target(d, p)
-            sib_out[d, p] = partial(z, 1 - core, h).astype(BF16)
-        for d in range(2):
-            sp_copy(d, p).start()
+            own = partial(z, core, h)
+            sp_copy(d, p).wait_recv()
+            mine[d, p] = own + sib_in[d, p].astype(F32)
 
     def rs_copy(d, p, v):
         return remote(
@@ -430,46 +468,55 @@
             nxt[d],
         )
 
-    def scatter_step(p, before):
-        mine = []
-        for d in range(2):
-            z, h = rs_target(d, p)
-            own = partial(z, core, h)
-            sp_copy(d, p).wait_recv()
-            mine.append(own + sib_in[d, p].astype(F32))
-        for v in range(2):
-            rows = quarter_of(v)
+    def pass_on(*slots):
+        for n in slots:
             for d in range(2):
-                block = mine[d][v * quarter : (v + 1) * quarter]
-                if before[d] is not None:
-                    rs_copy(d, before[d], v).wait_recv()
-                    block = block + rs_in[d, before[d], rows].astype(F32)
+                p, v = RS_ORDER[d][n]
+                rows = quarter_of(v)
+                block = mine[d, p, rows]
+                if p in RS_BEFORE[d]:
+                    before = RS_BEFORE[d][p]
+                    rs_copy(d, before, v).wait_recv()
+                    block = block + rs_in[d, before, rows].astype(F32)
                 rs_out[d, p, rows] = block.astype(BF16)
             for d in range(2):
+                p, v = RS_ORDER[d][n]
                 rs_copy(d, p, v).start()
 
-    def chained_step(p, carry):
-        scatter_step(p, (p - 2, p - 2))
-        return carry
-
+    activate(1 - zl)
     for_sibling(0)
+    prepare(0)
+    pass_on(0, 1)
+    take(items - 1)
+    for d, p in AG_WHOLE[items - 1]:
+        from_sibling(d, p)
+    activate(zl)
+
     for_sibling(1)
-    scatter_step(0, (None, None))
     for_sibling(2)
+    prepare(1)
+    pass_on(2, 3)
     for_sibling(3)
-    scatter_step(1, (0, None))
     for_sibling(4)
+    prepare(2)
+    pass_on(4)
     for_sibling(5)
-    scatter_step(2, (None, 0))
     for_sibling(6)
+    prepare(3)
+    pass_on(5, 6, 7)
     for h in range(2):
         sib_out[h, items] = partial(zeta, 1 - core, h).astype(BF16)
     for h in range(2):
         sp_copy(h, items).start()
-    lax.fori_loop(3, items, chained_step, 0)
-
-    def bk_copy(h, k):
-        to = lax.rem(exp + k, n_exp)
+    prepare(4)
+    pass_on(8, 9)
+    prepare(5)
+    pass_on(10)
+    prepare(6)
+    pass_on(11, 12, 13)
+
+    def bk_copy(h, offset):
+        to = partner(offset)
         return remote(back_out.at[h, to], back_in.at[h, exp], bk_send.at[h], bk_recv.at[h], {"exp": to})
 
     finals = [partial(zeta, core, h) for h in range(2)]
@@ -485,12 +532,8 @@
         dense = finals[h] + rs_in[0, p].astype(F32) + rs_in[1, p].astype(F32)
         to_blocks(back_out, h, dense.astype(BF16), blank)
         back_in[h, exp] = back_out[h, exp]
-
-        def bk_start(k, carry):
-            bk_copy(h, k).start()
-            return carry
-
-        lax.fori_loop(1, n_exp, bk_start, 0)
+        for offset in offsets:
+            bk_copy(h, offset).start()
 
     def sent(ref, sem):
         pltpu.make_async_copy(ref, ref, sem).wait()
@@ -574,6 +617,7 @@
             pltpu.VMEM((2, items + 1, half, width), BF16),
             pltpu.VMEM((2, items, half, width), BF16),
             pltpu.VMEM((2, items, half, width), BF16),
+            pltpu.VMEM((2, items, half, width), F32),
             blocks,
             blocks,
             dma((10,)),

time: 87.3 us -> 83.4 us (0.955)
  Pallas kernels: 85.5 us -> 81.5 us
    pallas_call x1, Pallas kernels: 85.5 us -> 81.5 us  [run_layer(): pl.pallas_call(kernel, out_shape=pltpu.VMEM((tokens, width), BF16), in_sp...]
where the time goes in v3:
time: 83.4 us; the launch traced here: 82.2 us
  Pallas kernels  81.5 us (98%)
    pallas_call x1, Pallas kernels, run_layer(): pl.pallas_call(kernel, out_shape=pltpu.VMEM((tokens, width), BF16), in_sp...  81.5 us

profile of v3, /device:TPU:6, one launch (start us, length us, event | category | flops | bytes accessed | tf_op | source)
XLA Modules:
  0.0 82.2 jit_solution(9038002955373079423)
XLA Ops:
  0.0 81.5 %layer.1 = bf16[128,640]{1,0:T(8,128)(2,1)S(1)} custom-call(bf16[128,128]{1,0:T(8,128)(2,1)} %bitcast.16, bf16[128,128]{1,0:T(8,128)(2,1)} %bitcast.17, s32[1,128]{1,0:T(1,128)} %bitcast.19, f32[1,128]{1,0:T(1,128)} %refs_3_.1, f32[5,128]{1,0:T(8,128)} %bitcast.18, bf16[128,640]{1,0:T(8,128)(2,1)} %bitcast.14, bf16[128,640]{1,0:T(8,128)(2,1)} %bitcast.15, ...), custom_call_target="tpu_custom_call" | custom-call | tf_op jit(solution)/shard_map/layer/pallas_call | solution.py:586
  81.6 0.7 copy.12
